TPU v7x, 32 devices: a whole 2x2x4 slice. The times are simulated.
32 devices in a mesh: pop: 16 (over z, x, core), hid: 2 (over y).
Axes of the slice: x: 2, y: 2, z: 4, core: 2. Of those that a mesh axis runs over, the one named last changes fastest.
Arguments:
- tokens: bfloat16 [512, 4096], P('pop', 'hid'), may hold values from -6 to 6
- fitness_ranks: int32 [32], replicated, may hold values from 0 to 31, each once
- gate_weight: bfloat16 [4096, 16384], P('hid', 'pop'), may hold values from -0.09375 to 0.09375
- up_weight: bfloat16 [4096, 16384], P('hid', 'pop'), may hold values from -0.09375 to 0.09375
- down_weight: bfloat16 [16384, 4096], P('pop', 'hid'), may hold values from -0.046875 to 0.046875
- gate_input_factor: bfloat16 [32, 4, 4096], P(None, None, 'hid'), may hold values from -6 to 6
- up_input_factor: bfloat16 [32, 4, 4096], P(None, None, 'hid'), may hold values from -6 to 6
- down_right: bfloat16 [32, 4, 4096], P(None, None, 'hid'), may hold values from -6 to 6
- gate_output_factor: bfloat16 [32, 4, 16384], P('pop'), may hold values from -6 to 6
- up_output_factor: bfloat16 [32, 4, 16384], P('pop'), may hold values from -6 to 6
- down_left: bfloat16 [32, 4, 16384], P('pop'), may hold values from -6 to 6
Outputs:
- mixed: bfloat16 [512, 4096], P('pop', 'hid')
- gate_step: float32 [4096, 16384], P('hid', 'pop')
- up_step: float32 [4096, 16384], P('hid', 'pop')
- down_step: float32 [16384, 4096], P('pop', 'hid')
Inputs may be any that keep to these rules, and one draw needn't show every extreme that they name: `fitness_ranks`: every rank appears exactly once.
All inputs are finite; a program needn't handle non-finite values.
Results may differ from a plain program's by a relative error of at most 0.025.
Values may be sent and summed in bfloat16 or wider, within the bound.
No kernel may reach another device: no remote copies, remote signals or barrier semaphores. Data moves between devices by JAX's collectives and lax.ppermute only.
A program may use at most 128 MiB of HBM per device.

v0:
```python
import math
import jax
import jax.numpy as jnp
from jax import lax
from jax.sharding import PartitionSpec as P

MODEL_WIDTH = 4096
HIDDEN_UNITS = 16384
RANK = 4
SAMPLE_LENGTH = 16


def local(
    tokens,
    fitness_ranks,
    gate_weight,
    up_weight,
    down_weight,
    gate_input_factor,
    up_input_factor,
    down_right,
    gate_output_factor,
    up_output_factor,
    down_left,
):
    scalar_real = jnp.float32
    pop_count = lax.axis_size("pop")
    hid_count = lax.axis_size("hid")
    pop_index = lax.axis_index("pop")
    hid_index = lax.axis_index("hid")
    tok_local = tokens.shape[0]
    mem_local = tok_local // SAMPLE_LENGTH
    members = mem_local * pop_count
    total_rows = tok_local * pop_count
    row_block_count = total_rows // hid_count
    block_members = row_block_count // SAMPLE_LENGTH
    width_part = tokens.shape[1]
    hidden_portion = gate_weight.shape[1]
    scale_in = 0.5 / math.sqrt(MODEL_WIDTH * RANK)
    scale_out = 0.5 / math.sqrt(HIDDEN_UNITS * RANK)
    fitness = fitness_ranks.astype(scalar_real) / (members - 1) - 0.5
    member_token_rows = tokens.reshape(mem_local, SAMPLE_LENGTH, width_part)
    member_gate_input = lax.dynamic_slice_in_dim(
        gate_input_factor, pop_index * mem_local, mem_local, 0
    )
    member_up_input = lax.dynamic_slice_in_dim(up_input_factor, pop_index * mem_local, mem_local, 0)
    gate_projection = jnp.einsum(
        "otl,ozl->otz", member_token_rows, member_gate_input, preferred_element_type=scalar_real
    )
    up_projection = jnp.einsum(
        "otl,ozl->otz", member_token_rows, member_up_input, preferred_element_type=scalar_real
    )
    gate_projection, up_projection = lax.psum((gate_projection, up_projection), "hid")
    gate_projection, up_projection = (
        lax.all_gather(gate_projection, "pop", axis=0, tiled=True),
        lax.all_gather(up_projection, "pop", axis=0, tiled=True),
    )
    gate_cols, up_cols, down_cols = (
        lax.all_to_all(gate_output_factor, "pop", split_axis=2, concat_axis=0, tiled=True),
        lax.all_to_all(up_output_factor, "pop", split_axis=2, concat_axis=0, tiled=True),
        lax.all_to_all(down_left, "pop", split_axis=2, concat_axis=0, tiled=True),
    )
    gathered = lax.all_gather(tokens, "pop", axis=0, tiled=True)
    paired = jnp.concatenate([gate_weight, up_weight], axis=1)
    picked = gathered
    sums = lax.psum_scatter(
        jnp.dot(picked, paired, preferred_element_type=scalar_real).astype(jnp.bfloat16),
        "hid",
        scatter_dimension=0,
        tiled=True,
    ).astype(jnp.float32)
    gate_sum = sums[:, :hidden_portion]
    up_sum = sums[:, hidden_portion:]
    first_member = hid_index * block_members
    gate_tile_block = lax.dynamic_slice_in_dim(gate_projection, first_member, block_members, 0)
    up_tile_block = lax.dynamic_slice_in_dim(up_projection, first_member, block_members, 0)
    gate_vectors = lax.dynamic_slice_in_dim(gate_cols, first_member, block_members, 0).astype(
        scalar_real
    )
    up_vectors = lax.dynamic_slice_in_dim(up_cols, first_member, block_members, 0).astype(
        scalar_real
    )
    gate_lowrank_term = jnp.einsum("iln,ina->ila", gate_tile_block, gate_vectors).reshape(
        row_block_count, hidden_portion
    )
    up_lowrank_term = jnp.einsum("iln,ina->ila", up_tile_block, up_vectors).reshape(
        row_block_count, hidden_portion
    )
    gate = gate_sum + scale_in * gate_lowrank_term
    up = up_sum + scale_in * up_lowrank_term
    hidden = (jax.nn.silu(gate) * up).astype(jnp.bfloat16)
    every_hidden = lax.all_gather(hidden, "hid", axis=0, tiled=True)
    picked = every_hidden
    member_count = lax.axis_size("pop") * tok_local // SAMPLE_LENGTH
    output_factor_portion = down_right.astype(scalar_real)
    contracting_matrix = jnp.einsum(
        "reu,ryu->rey",
        picked.reshape(member_count, SAMPLE_LENGTH, hidden_portion),
        down_cols,
        preferred_element_type=scalar_real,
    )
    lowrank_product = jnp.einsum("okw,owt->okt", contracting_matrix, output_factor_portion).reshape(
        lax.axis_size("pop") * tok_local, width_part
    )
    mixed = lax.psum_scatter(
        (
            jnp.dot(picked, down_weight, preferred_element_type=scalar_real)
            + scale_out * lowrank_product
        ).astype(jnp.bfloat16),
        "pop",
        scatter_dimension=0,
        tiled=True,
    )
    factor = 1.0 / math.sqrt(members * RANK)
    weights3 = fitness[:, None, None]
    scaled_gate = (
        (gate_input_factor.astype(scalar_real) * weights3)
        .astype(jnp.bfloat16)
        .reshape(members * RANK, width_part)
    )
    scaled_up = (
        (up_input_factor.astype(scalar_real) * weights3)
        .astype(jnp.bfloat16)
        .reshape(members * RANK, width_part)
    )
    scaled_down = (
        (down_right.astype(scalar_real) * weights3)
        .astype(jnp.bfloat16)
        .reshape(members * RANK, width_part)
    )
    dims = (((0,), (0,)), ((), ()))
    gate_step = factor * lax.dot_general(
        scaled_gate,
        gate_cols.reshape(members * RANK, hidden_portion),
        dims,
        preferred_element_type=scalar_real,
    )
    up_step = factor * lax.dot_general(
        scaled_up,
        up_cols.reshape(members * RANK, hidden_portion),
        dims,
        preferred_element_type=scalar_real,
    )
    down_step = factor * lax.dot_general(
        down_cols.reshape(members * RANK, hidden_portion),
        scaled_down,
        dims,
        preferred_element_type=scalar_real,
    )
    return (mixed, gate_step, up_step, down_step)


def solution(mesh):
    in_specs = (
        P("pop", "hid"),
        P(),
        P("hid", "pop"),
        P("hid", "pop"),
        P("pop", "hid"),
        P(None, None, "hid"),
        P(None, None, "hid"),
        P(None, None, "hid"),
        P("pop", None, None),
        P("pop", None, None),
        P("pop", None, None),
    )
    out_specs = (P("pop", "hid"), P("hid", "pop"), P("hid", "pop"), P("pop", "hid"))
    return jax.shard_map(local, mesh=mesh, in_specs=in_specs, out_specs=out_specs, check_vma=False)
```

profile of v0, /device:TPU:0, one launch (start us, length us, event | category | flops | bytes accessed | tf_op | source)
XLA Modules:
  0.0 419.8 jit_solution(13870929993239631916)
XLA Ops:
  7.2 0.0 all-gather.3.cloned.1.call-start
  7.2 0.7 all-gather.3.cloned.1.call-update
  7.9 0.0 copy-start.5
  7.9 0.0 reduce-scatter.3.cloned.1.call-start
  8.0 46.4 %all-gather.3.cloned.1.call-done = bf16[512,2048]{1,0:T(8,128)(2,1)} async-done(((bf16[32,2048]{1,0:T(8,128)(2,1)}), bf16[512,2048]{1,0:T(8,128)(2,1)}) %all-gather.3.cloned.1.call-update) | async-done | bytes 2097168 | tf_op jit(solution)/shard_map/all_gather | solution.py:63
  54.3 10.0 %fusion.8 = bf16[512,2048]{0,1:T(8,128)(2,1)} fusion(bf16[512,2048]{1,0:T(8,128)(2,1)} %all-gather.3.cloned.1.call-done, bf16[2048,1024]{1,0:T(8,128)(2,1)} %param.14, bf16[2048,1024]{1,0:T(8,128)(2,1)} %param.13), kind=kOutput, calls=%fused_computation.11 | convolution fusion | flops 4312793088 | bytes 12582912 | tf_op jit(solution)/shard_map/dot_general | solution.py:67
  64.3 0.0 reduce-scatter.3.cloned.1.call-update
  64.3 0.0 copy-done.5
  64.3 13.0 %copy.27 = bf16[2,4,16384]{1,0,2:T(2,128)(2,1)} copy(bf16[2,4,16384]{2,1,0:T(4,128)(2,1)S(1)} %copy-done.5) | data formatting | bytes 524288 | tf_op args[8]
  77.3 16.9 %reshape.55 = bf16[16,2,4096]{2,1,0:T(2,128)(2,1)} reshape(bf16[16384,2,4]{2,1,0:T(2,128)(2,1)} %bitcast.51) | data formatting | bytes 524288
  94.2 3.5 all-to-all-start
  97.7 0.0 copy-done.6
  97.7 13.0 %copy.30 = bf16[2,4,16384]{1,0,2:T(2,128)(2,1)} copy(bf16[2,4,16384]{2,1,0:T(4,128)(2,1)S(1)} %copy-done.6) | data formatting | bytes 524288 | tf_op args[9]
  110.7 16.9 %reshape.53 = bf16[16,2,4096]{2,1,0:T(2,128)(2,1)} reshape(bf16[16384,2,4]{2,1,0:T(2,128)(2,1)} %bitcast.52) | data formatting | bytes 524288
  127.5 0.0 all-to-all-done
  127.5 6.0 %all-to-all-start.1 = ((bf16[16,2,4096]{2,1,0:T(2,128)(2,1)}), bf16[16,2,4096]{2,1,0:T(2,128)(2,1)S(1)}, u32[]{:S(2)}, u32[]{:S(2)}) async-start(bf16[16,2,4096]{2,1,0:T(2,128)(2,1)} %reshape.53), calls=%async_computation.2 | async-start | bytes 524288 | tf_op jit(solution)/shard_map/all_to_all | solution.py:60
  133.5 0.0 all-gather.5.cloned.1.call-start
  133.6 0.0 copy-done.4
  133.6 0.9 convolution_bitcast_fusion
  134.5 0.9 convolution_bitcast_fusion.1
  135.4 5.0 %all-reduce = (bf16[2,16,4]{1,2,0:T(4,128)(2,1)S(1)}, bf16[2,16,4]{1,2,0:T(4,128)(2,1)S(1)}) all-reduce(f32[2,16,4]{1,2,0:T(4,128)S(1)} %convolution_bitcast_fusion, f32[2,16,4]{1,2,0:T(4,128)S(1)} %convolution_bitcast_fusion.1), channel_id=1, replica_groups=mesh['pop'=16,'hid'=2] {'hid'}, use_global_device_ids=true, to_apply=%region_2.0 | all-reduce | flops 256 | bytes 1536 | tf_op jit(solution)/shard_map/psum | solution.py:53
  140.4 21.8 %all_gather.13 = bf16[32,16,4]{1,2,0:T(4,128)(2,1)S(1)} all-gather(bf16[2,16,4]{1,2,0:T(4,128)(2,1)S(1)} %get-tuple-element.17), channel_id=1, replica_groups=mesh['pop'=16,'hid'=2] {'pop'}, dimensions={0}, use_global_device_ids=true | all-gather | bytes 4352 | tf_op jit(solution)/shard_map/all_gather | solution.py:55
  162.2 17.7 %all_gather.14 = bf16[32,16,4]{1,2,0:T(4,128)(2,1)S(1)} all-gather(bf16[2,16,4]{1,2,0:T(4,128)(2,1)S(1)} %get-tuple-element.16), channel_id=1, replica_groups=mesh['pop'=16,'hid'=2] {'pop'}, dimensions={0}, use_global_device_ids=true | all-gather | bytes 4352 | tf_op jit(solution)/shard_map/all_gather | solution.py:56
  179.8 19.0 %reshape.56 = bf16[16384,2,4]{2,1,0:T(2,128)(2,1)} reshape(bf16[16,2,4096]{2,1,0:T(2,128)(2,1)S(1)} %all-to-all-done) | data formatting | bytes 524288
  198.9 19.2 %copy.28 = bf16[2,4,16,1024]{3,1,0,2:T(4,128)(2,1)S(1)} copy(bf16[2,4,16,1024]{1,0,3,2:T(2,128)(2,1)} %bitcast.48) | data formatting | bytes 524288 | tf_op jit(solution)/shard_map/all_to_all | solution.py:59
  218.0 0.4 convolution_multiply_fusion.4
  218.4 0.3 copy.29
  218.8 0.0 all-to-all-done.1
  218.8 19.1 %reshape.54 = bf16[16384,2,4]{2,1,0:T(2,128)(2,1)} reshape(bf16[16,2,4096]{2,1,0:T(2,128)(2,1)S(1)} %all-to-all-done.1) | data formatting | bytes 524288
  237.8 19.2 %copy.31 = bf16[2,4,16,1024]{3,1,0,2:T(4,128)(2,1)S(1)} copy(bf16[2,4,16,1024]{1,0,3,2:T(2,128)(2,1)} %bitcast.49) | data formatting | bytes 524288 | tf_op jit(solution)/shard_map/all_to_all | solution.py:60
  257.0 0.0 copy-start.2
  257.0 0.4 convolution_multiply_fusion.3
  257.4 0.3 copy-done.2
  257.7 0.3 copy.32
  258.1 0.0 copy-start.7
  258.1 0.0 reduce-scatter.3.cloned.1.call-done
  258.1 1.4 convert_element_type.41
  259.5 1.2 fusion.14
  260.8 0.0 all-gather.5.cloned.1.call-update
  260.8 0.0 reduce-scatter.5.cloned.1.call-start
  260.8 0.0 copy-done.7
  260.8 13.0 %copy.34 = bf16[2,4,16384]{1,0,2:T(2,128)(2,1)} copy(bf16[2,4,16384]{2,1,0:T(4,128)(2,1)S(1)} %copy-done.7) | data formatting | bytes 524288 | tf_op args[10]
  273.8 16.2 %reshape.57 = bf16[16,2,4096]{2,1,0:T(2,128)(2,1)S(1)} reshape(bf16[16384,2,4]{2,1,0:T(2,128)(2,1)} %bitcast.53) | data formatting | bytes 524288
  290.0 12.9 %all_to_all.54 = bf16[16,2,4096]{2,1,0:T(2,128)(2,1)S(1)} all-to-all(bf16[16,2,4096]{2,1,0:T(2,128)(2,1)S(1)} %reshape.57), channel_id=1, replica_groups=mesh['pop'=16,'hid'=2] {'pop'}, dimensions={0} | all-to-all | bytes 524288 | tf_op jit(solution)/shard_map/all_to_all | solution.py:61
  302.9 19.0 %reshape.58 = bf16[16384,2,4]{2,1,0:T(2,128)(2,1)} reshape(bf16[16,2,4096]{2,1,0:T(2,128)(2,1)S(1)} %all_to_all.54) | data formatting | bytes 524288
  321.9 19.2 %copy.35 = bf16[2,4,16,1024]{3,1,0,2:T(4,128)(2,1)S(1)} copy(bf16[2,4,16,1024]{1,0,3,2:T(2,128)(2,1)} %bitcast.50) | data formatting | bytes 524288 | tf_op jit(solution)/shard_map/all_to_all | solution.py:61
  341.2 0.0 all-gather.5.cloned.1.call-done
  341.2 0.0 copy-start
  341.2 1.6 copy.33
  342.8 3.1 convolution_multiply_fusion.2
  345.9 7.2 %fusion.4 = bf16[512,2048]{1,0:T(8,128)(2,1)} fusion(f32[32,16,2048]{2,1,0:T(8,128)} %convolution_multiply_fusion.2, bf16[512,1024]{0,1:T(8,128)(2,1)S(1)} %copy-done, bf16[1024,2048]{1,0:T(8,128)(2,1)} %param.15), kind=kOutput, calls=%fused_computation.8 | convolution fusion | flops 2149580800 | bytes 11534336 | tf_op jit(solution)/shard_map/dot_general | solution.py:107
  353.1 0.0 reduce-scatter.5.cloned.1.call-update
  353.1 2.3 multiply_convert_fusion
  355.4 0.1 reshape.51
  355.5 0.1 reshape.49
  355.6 0.1 reshape.47
  355.8 0.1 reshape.52
  355.8 4.7 %multiply_bitcast_fusion = f32[1024,2048]{0,1:T(8,128)} fusion(bf16[128,2048]{1,0:T(8,128)(2,1)S(1)} %reshape.51, bf16[128,1024]{1,0:T(8,128)(2,1)S(1)} %reshape.52), kind=kOutput, calls=%fused_computation.4 | convolution fusion | flops 538968064 | bytes 9175040 | tf_op jit(solution)/shard_map/dot_general | solution.py:144
  360.5 9.3 %copy.36 = f32[1024,2048]{1,0:T(8,128)} copy(f32[1024,2048]{0,1:T(8,128)} %multiply_bitcast_fusion) | data formatting | bytes 16777216
  369.8 0.1 reshape.50
  369.9 0.1 reshape.48
  370.0 4.7 %convolution_multiply_fusion = f32[2048,1024]{1,0:T(8,128)} fusion(bf16[128,2048]{1,0:T(8,128)(2,1)S(1)} %reshape.49, bf16[128,1024]{1,0:T(8,128)(2,1)S(1)} %reshape.50), kind=kOutput, calls=%fused_computation.5 | convolution fusion | flops 538968064 | bytes 9175040 | tf_op jit(solution)/shard_map/dot_general | solution.py:138
  374.6 4.7 %convolution_multiply_fusion.1 = f32[2048,1024]{1,0:T(8,128)} fusion(bf16[128,2048]{1,0:T(8,128)(2,1)S(1)} %reshape.47, bf16[128,1024]{1,0:T(8,128)(2,1)S(1)} %reshape.48), kind=kOutput, calls=%fused_computation.6 | convolution fusion | flops 538968064 | bytes 9175040 | tf_op jit(solution)/shard_map/dot_general | solution.py:132
  379.3 33.9 %reduce-scatter.5.cloned.1.call-done = bf16[32,2048]{1,0:T(8,128)(2,1)} async-done(((bf16[512,2048]{1,0:T(8,128)(2,1)}), bf16[32,2048]{1,0:T(8,128)(2,1)}) %reduce-scatter.5.cloned.1.call-update) | async-done | bytes 131088 | tf_op jit(solution)/shard_map/reduce_scatter | solution.py:105
  (10 shorter events, 0.0 us)
Async XLA Ops:
  7.2 47.2 %all-gather.3.cloned.1.call-start = ((), (), s32[]{:S(2)}) async-start(), calls=%async_computation.5 | async-start | bytes 2228224 | tf_op jit(solution)/shard_map/all_gather | solution.py:63
  7.9 56.4 %copy-start.5 = (bf16[2,4,16384]{2,1,0:T(4,128)(2,1)S(1)}, bf16[2,4,16384]{2,1,0:T(4,128)(2,1)}, u32[]{:S(2)}) copy-start(bf16[2,4,16384]{2,1,0:T(4,128)(2,1)} %param.19) | copy-start | bytes 786436
  7.9 250.2 %reduce-scatter.3.cloned.1.call-start = ((), (), s32[]{:S(2)}) async-start(), calls=%async_computation.6 | async-start | bytes 3145728 | tf_op jit(solution)/shard_map/reduce_scatter | solution.py:66
  77.3 20.4 %copy-start.6 = (bf16[2,4,16384]{2,1,0:T(4,128)(2,1)S(1)}, bf16[2,4,16384]{2,1,0:T(4,128)(2,1)}, u32[]{:S(2)}) copy-start(bf16[2,4,16384]{2,1,0:T(4,128)(2,1)} %param.20) | copy-start | bytes 786436
  94.2 33.4 %all-to-all-start = ((bf16[16,2,4096]{2,1,0:T(2,128)(2,1)}), bf16[16,2,4096]{2,1,0:T(2,128)(2,1)S(1)}, u32[]{:S(2)}, u32[]{:S(2)}) async-start(bf16[16,2,4096]{2,1,0:T(2,128)(2,1)} %reshape.55), calls=%async_computation.1 | async-start | bytes 524288 | tf_op jit(solution)/shard_map/all_to_all | solution.py:59
  110.7 22.9 %copy-start.4 = (bf16[32,2048]{1,0:T(8,128)(2,1)S(1)}, bf16[32,2048]{1,0:T(8,128)(2,1)}, u32[]{:S(2)}) copy-start(bf16[32,2048]{1,0:T(8,128)(2,1)} %param.11) | copy-start | bytes 393220
  127.5 91.2 %all-to-all-start.1 = ((bf16[16,2,4096]{2,1,0:T(2,128)(2,1)}), bf16[16,2,4096]{2,1,0:T(2,128)(2,1)S(1)}, u32[]{:S(2)}, u32[]{:S(2)}) async-start(bf16[16,2,4096]{2,1,0:T(2,128)(2,1)} %reshape.53), calls=%async_computation.2 | async-start | bytes 524288 | tf_op jit(solution)/shard_map/all_to_all | solution.py:60
  133.5 207.7 %all-gather.5.cloned.1.call-start = ((), (), s32[]{:S(2)}) async-start(), calls=%async_computation.7 | async-start | bytes 1572864 | tf_op jit(solution)/shard_map/all_gather | solution.py:92
  257.0 0.7 copy-start.2
  258.1 2.8 copy-start.7
  260.8 152.5 %reduce-scatter.5.cloned.1.call-start = ((), (), s32[]{:S(2)}) async-start(), calls=%async_computation.8 | async-start | bytes 2228224 | tf_op jit(solution)/shard_map/reduce_scatter | solution.py:105
  321.9 20.9 %copy-start.1 = (bf16[32,4,2048]{2,1,0:T(4,128)(2,1)S(1)}, bf16[32,4,2048]{2,1,0:T(4,128)(2,1)}, u32[]{:S(2)}) copy-start(bf16[32,4,2048]{2,1,0:T(4,128)(2,1)} %param.18) | copy-start | bytes 1572868
  341.2 4.7 %copy-start = (bf16[512,1024]{0,1:T(8,128)(2,1)S(1)}, bf16[512,1024]{0,1:T(8,128)(2,1)}, u32[]{:S(2)}) copy-start(bf16[512,1024]{0,1:T(8,128)(2,1)} %all-gather.5.cloned.1.call-done) | copy-start | bytes 3145732
  345.9 7.2 %copy-start.8 = (s32[32]{0:T(128)S(1)}, s32[32]{0:T(128)}, u32[]{:S(2)}) copy-start(s32[32]{0:T(128)} %param.12) | copy-start | bytes 388
  360.5 9.3 %copy-start.3 = (bf16[2,4,16,1024]{3,1,0,2:T(4,128)(2,1)S(1)}, bf16[2,4,16,1024]{3,1,0,2:T(4,128)(2,1)}, u32[]{:S(2)}) copy-start(bf16[2,4,16,1024]{3,1,0,2:T(4,128)(2,1)} %copy-done.2) | copy-start | bytes 786436
Sparse Core Ops, SparseCore 0:
  10.1 44.1 all-gather.2
  64.5 30.6 reduce-scatter.2
  260.9 19.5 all-gather.4
  353.2 59.9 reduce-scatter.4
where the time goes:
time: 422 us; the launch traced here: 420 us
  local copies, waits for them, and re-layouts  216 us (51%)
  waiting for transfers between devices  81.1 us (19%)
  blocking collectives  57.3 us (14%)
  matrix products  36.8 us (9%)
  between operations  14 us (3%)
  starting transfers between devices  9.65 us (2%)
  other arithmetic  4.9 us (1%)
    unnamed x28, local copies, waits for them, and re-layouts  156 us
    all_gather x1, waiting for transfers between devices, local(): gathered = lax.all_gather(tokens, 'pop', axis=0, tiled=True)  46.4 us
    reduce_scatter x1, waiting for transfers between devices, local(): lax.psum_scatter((jnp.dot(picked, down_weight, preferred_element_type=sca...  33.9 us
    all_gather x1, blocking collectives, local(): lax.all_gather(gate_projection, 'pop', axis=0, tiled=True)  21.8 us
    all_to_all x1, local copies, waits for them, and re-layouts, local(): lax.all_to_all(down_left, 'pop', split_axis=2, concat_axis=0, tiled=True)  19.2 us
    all_to_all x1, local copies, waits for them, and re-layouts, local(): lax.all_to_all(gate_output_factor, 'pop', split_axis=2, concat_axis=0, ti...  19.2 us
    all_to_all x1, local copies, waits for them, and re-layouts, local(): lax.all_to_all(up_output_factor, 'pop', split_axis=2, concat_axis=0, tile...  19.2 us
    all_gather x1, blocking collectives, local(): lax.all_gather(up_projection, 'pop', axis=0, tiled=True)  17.7 us
  transfers between devices with their start and end apart: 6, of which 2 were waited for; matrix products, arithmetic and copies ran while one was open for 55% of the time, Pallas kernels for 0%

commit v1 on v0

--- a/solution.py
+++ b/solution.py
@@ -8,6 +8,12 @@
 HIDDEN_UNITS = 16384
 RANK = 4
 SAMPLE_LENGTH = 16
+
+
+def stacked_exchange(x, mesh_axis, split, join):
+    parts = jnp.split(x, lax.axis_size(mesh_axis), axis=split)
+    received = lax.all_to_all(jnp.stack(parts), mesh_axis, 0, 0)
+    return jnp.concatenate(received, axis=join)
 
 
 def local(
@@ -58,7 +64,7 @@
     gate_cols, up_cols, down_cols = (
         lax.all_to_all(gate_output_factor, "pop", split_axis=2, concat_axis=0, tiled=True),
         lax.all_to_all(up_output_factor, "pop", split_axis=2, concat_axis=0, tiled=True),
-        lax.all_to_all(down_left, "pop", split_axis=2, concat_axis=0, tiled=True),
+        stacked_exchange(down_left, "pop", 2, 0),
     )
     gathered = lax.all_gather(tokens, "pop", axis=0, tiled=True)
     paired = jnp.concatenate([gate_weight, up_weight], axis=1)

time: 422 us -> 372 us (0.88)
  local copies, waits for them, and re-layouts: 216 us -> 151 us
  waiting for transfers between devices: 81.1 us -> 105 us
  blocking collectives: 57.3 us -> 44.2 us
    unnamed x28 -> x41, local copies, waits for them, and re-layouts: 156 us -> 109 us
    all_to_all x1 -> x0, local copies, waits for them, and re-layouts: 19.2 us -> none  [local(): lax.all_to_all(down_left, 'pop', split_axis=2, concat_axis=0, tiled=True)]
    all_to_all x1 -> x0, blocking collectives: 12.9 us -> none  [local(): lax.all_to_all(down_left, 'pop', split_axis=2, concat_axis=0, tiled=True)]
    all_gather x1, waiting for transfers between devices: 0.02 us -> 12.7 us  [local(): every_hidden = lax.all_gather(hidden, 'hid', axis=0, tiled=True)]
    reduce_scatter x1, waiting for transfers between devices: 33.9 us -> 45 us  [local(): lax.psum_scatter((jnp.dot(picked, down_weight, preferred_element_type=sca...]
    all_to_all x0 -> x1, starting transfers between devices: none -> 5.97 us  [stacked_exchange(): received = lax.all_to_all(jnp.stack(parts), mesh_axis, 0, 0)]
  transfers between devices with their start and end apart: 6 -> 7, of which waited for: 2 -> 3; matrix products, arithmetic and copies ran while one was open for 55% -> 46% of each run, Pallas kernels for 0% -> 0%
where the time goes in v1:
time: 372 us; the launch traced here: 370 us
  local copies, waits for them, and re-layouts  151 us (41%)
  waiting for transfers between devices  105 us (28%)
  blocking collectives  44.2 us (12%)
  matrix products  37.9 us (10%)
  between operations  14 us (4%)
  starting transfers between devices  13.4 us (4%)
  other arithmetic  4.88 us (1%)
    unnamed x41, local copies, waits for them, and re-layouts  109 us
    all_gather x1, waiting for transfers between devices, local(): gathered = lax.all_gather(tokens, 'pop', axis=0, tiled=True)  46.4 us
    reduce_scatter x1, waiting for transfers between devices, local(): lax.psum_scatter((jnp.dot(picked, down_weight, preferred_element_type=sca...  45 us
    all_gather x1, blocking collectives, local(): lax.all_gather(gate_projection, 'pop', axis=0, tiled=True)  21.7 us
    all_to_all x1, local copies, waits for them, and re-layouts, local(): lax.all_to_all(gate_output_factor, 'pop', split_axis=2, concat_axis=0, ti...  19.2 us
    all_to_all x1, local copies, waits for them, and re-layouts, local(): lax.all_to_all(up_output_factor, 'pop', split_axis=2, concat_axis=0, tile...  19.2 us
    all_gather x1, blocking collectives, local(): lax.all_gather(up_projection, 'pop', axis=0, tiled=True)  17.5 us
    all_gather x1, waiting for transfers between devices, local(): every_hidden = lax.all_gather(hidden, 'hid', axis=0, tiled=True)  12.7 us
  transfers between devices with their start and end apart: 7, of which 3 were waited for; matrix products, arithmetic and copies ran while one was open for 46% of the time, Pallas kernels for 0%

profile of v1, /device:TPU:0, one launch (start us, length us, event | category | flops | bytes accessed | tf_op | source)
XLA Modules:
  0.0 370.2 jit_solution(18268467448176289488)
XLA Ops:
  7.2 0.0 all-gather.3.cloned.1.call-start
  7.2 0.7 all-gather.3.cloned.1.call-update
  7.9 0.0 reduce-scatter.3.cloned.1.call-start
  8.0 46.4 %all-gather.3.cloned.1.call-done = bf16[512,2048]{1,0:T(8,128)(2,1)} async-done(((bf16[32,2048]{1,0:T(8,128)(2,1)}), bf16[512,2048]{1,0:T(8,128)(2,1)}) %all-gather.3.cloned.1.call-update) | async-done | bytes 2097168 | tf_op jit(solution)/shard_map/all_gather | solution.py:69
  54.3 10.0 %fusion.8 = bf16[512,2048]{0,1:T(8,128)(2,1)} fusion(bf16[512,2048]{1,0:T(8,128)(2,1)} %all-gather.3.cloned.1.call-done, bf16[2048,1024]{1,0:T(8,128)(2,1)} %param.14, bf16[2048,1024]{1,0:T(8,128)(2,1)} %param.13), kind=kOutput, calls=%fused_computation.11 | convolution fusion | flops 4312793088 | bytes 12582912 | tf_op jit(solution)/shard_map/dot_general | solution.py:73
  64.3 0.0 reduce-scatter.3.cloned.1.call-update
  64.3 13.0 %copy.24 = bf16[2,4,16384]{1,0,2:T(2,128)(2,1)} copy(bf16[2,4,16384]{2,1,0:T(4,128)(2,1)S(1)} %copy-done.6) | data formatting | bytes 524288 | tf_op args[8]
  77.3 16.9 %reshape.54 = bf16[16,2,4096]{2,1,0:T(2,128)(2,1)} reshape(bf16[16384,2,4]{2,1,0:T(2,128)(2,1)} %bitcast.75) | data formatting | bytes 524288
  94.2 3.5 all-to-all-start
  97.7 0.6 constant_dynamic-update-slice_fusion.15
  98.4 0.6 constant_dynamic-update-slice_fusion.14
  99.0 0.6 constant_dynamic-update-slice_fusion.13
  99.6 0.6 constant_dynamic-update-slice_fusion.12
  100.2 0.6 constant_dynamic-update-slice_fusion.11
  100.8 0.6 constant_dynamic-update-slice_fusion.10
  101.4 0.6 constant_dynamic-update-slice_fusion.9
  102.0 0.6 constant_dynamic-update-slice_fusion.8
  102.6 0.9 convolution_bitcast_fusion
  103.5 0.9 convolution_bitcast_fusion.1
  104.4 0.6 constant_dynamic-update-slice_fusion.7
  105.0 12.9 %copy.27 = bf16[2,4,16384]{1,0,2:T(2,128)(2,1)} copy(bf16[2,4,16384]{2,1,0:T(4,128)(2,1)S(1)} %copy-done.7) | data formatting | bytes 524288 | tf_op args[9]
  117.9 16.8 %reshape.52 = bf16[16,2,4096]{2,1,0:T(2,128)(2,1)} reshape(bf16[16384,2,4]{2,1,0:T(2,128)(2,1)} %bitcast.76) | data formatting | bytes 524288
  134.8 5.0 %all-reduce = (bf16[2,16,4]{1,2,0:T(4,128)(2,1)S(1)}, bf16[2,16,4]{1,2,0:T(4,128)(2,1)S(1)}) all-reduce(f32[2,16,4]{1,2,0:T(4,128)S(1)} %convolution_bitcast_fusion, f32[2,16,4]{1,2,0:T(4,128)S(1)} %convolution_bitcast_fusion.1), channel_id=1, replica_groups=mesh['pop'=16,'hid'=2] {'hid'}, use_global_device_ids=true, to_apply=%region_2.0 | all-reduce | flops 256 | bytes 1536 | tf_op jit(solution)/shard_map/psum | solution.py:59
  139.7 21.7 %all_gather.13 = bf16[32,16,4]{1,2,0:T(4,128)(2,1)S(1)} all-gather(bf16[2,16,4]{1,2,0:T(4,128)(2,1)S(1)} %get-tuple-element.5), channel_id=1, replica_groups=mesh['pop'=16,'hid'=2] {'pop'}, dimensions={0}, use_global_device_ids=true | all-gather | bytes 4352 | tf_op jit(solution)/shard_map/all_gather | solution.py:61
  161.4 17.5 %all_gather.14 = bf16[32,16,4]{1,2,0:T(4,128)(2,1)S(1)} all-gather(bf16[2,16,4]{1,2,0:T(4,128)(2,1)S(1)} %get-tuple-element.4), channel_id=1, replica_groups=mesh['pop'=16,'hid'=2] {'pop'}, dimensions={0}, use_global_device_ids=true | all-gather | bytes 4352 | tf_op jit(solution)/shard_map/all_gather | solution.py:62
  178.9 0.6 constant_dynamic-update-slice_fusion.6
  179.6 0.6 constant_dynamic-update-slice_fusion.5
  180.2 3.5 all-to-all-start.1
  183.7 0.2 all-gather.5.cloned.1.call-start
  183.9 0.6 constant_dynamic-update-slice_fusion.4
  184.5 0.6 constant_dynamic-update-slice_fusion.3
  185.1 19.0 %reshape.55 = bf16[16384,2,4]{2,1,0:T(2,128)(2,1)} reshape(bf16[16,2,4096]{2,1,0:T(2,128)(2,1)S(1)} %all-to-all-done) | data formatting | bytes 524288
  204.2 19.2 %copy.25 = bf16[2,4,16,1024]{3,1,0,2:T(4,128)(2,1)S(1)} copy(bf16[2,4,16,1024]{1,0,3,2:T(2,128)(2,1)} %bitcast.73) | data formatting | bytes 524288 | tf_op jit(solution)/shard_map/all_to_all | solution.py:65
  223.4 0.4 convolution_multiply_fusion.5
  223.7 0.3 copy.26
  224.1 19.1 %reshape.53 = bf16[16384,2,4]{2,1,0:T(2,128)(2,1)} reshape(bf16[16,2,4096]{2,1,0:T(2,128)(2,1)S(1)} %all-to-all-done.1) | data formatting | bytes 524288
  243.2 19.2 %copy.28 = bf16[2,4,16,1024]{3,1,0,2:T(4,128)(2,1)S(1)} copy(bf16[2,4,16,1024]{1,0,3,2:T(2,128)(2,1)} %bitcast.74) | data formatting | bytes 524288 | tf_op jit(solution)/shard_map/all_to_all | solution.py:66
  262.3 0.4 convolution_multiply_fusion.4
  262.7 0.3 copy-done.2
  263.0 0.3 copy.29
  263.4 0.0 reduce-scatter.3.cloned.1.call-done
  263.4 1.4 convert_element_type.41
  264.8 1.2 fusion.14
  266.0 0.0 all-gather.5.cloned.1.call-update
  266.0 1.3 constant_dynamic-update-slice_fusion.2
  267.4 1.3 constant_dynamic-update-slice_fusion.1
  268.7 1.3 constant_dynamic-update-slice_fusion
  270.0 6.0 %all-to-all-start.2 = ((bf16[16,2,4,1024]{3,2,1,0:T(4,128)(2,1)}), bf16[16,2,4,1024]{3,2,1,0:T(4,128)(2,1)S(1)}, u32[]{:S(2)}, u32[]{:S(2)}) async-start(bf16[16,2,4,1024]{3,2,1,0:T(4,128)(2,1)} %constant_dynamic-update-slice_fusion), calls=%async_computation.3 | async-start | bytes 524288 | tf_op jit(solution)/shard_map/all_to_all | solution.py:15
  276.0 0.0 reduce-scatter.5.cloned.1.call-start
  276.0 12.7 %all-gather.5.cloned.1.call-done = bf16[512,1024]{0,1:T(8,128)(2,1)} async-done(((bf16[256,1024]{0,1:T(8,128)(2,1)}), bf16[512,1024]{0,1:T(8,128)(2,1)}) %all-gather.5.cloned.1.call-update) | async-done | bytes 1048592 | tf_op jit(solution)/shard_map/all_gather | solution.py:98
  288.7 1.6 copy.30
  290.3 4.1 %convolution_multiply_fusion.3 = f32[32,16,2048]{2,1,0:T(8,128)} fusion(bf16[32,4,2048]{2,1,0:T(4,128)(2,1)} %param.18, bf16[32,16,1024]{2,1,0:T(8,128)(2,1)S(1)} %bitcast.79, bf16[32,4,1024]{2,1,0:T(4,128)(2,1)S(1)} %bitcast.80), kind=kOutput, calls=%fused_computation.9 | convolution fusion | flops 13631488 | bytes 6029312 | tf_op jit(solution)/shard_map/okw,owt->okt/dot_general | solution.py:108
  294.5 7.2 %fusion.4 = bf16[512,2048]{1,0:T(8,128)(2,1)} fusion(f32[32,16,2048]{2,1,0:T(8,128)} %convolution_multiply_fusion.3, bf16[512,1024]{0,1:T(8,128)(2,1)S(1)} %copy-done, bf16[1024,2048]{1,0:T(8,128)(2,1)} %param.15), kind=kOutput, calls=%fused_computation.8 | convolution fusion | flops 2149580800 | bytes 11534336 | tf_op jit(solution)/shard_map/dot_general | solution.py:113
  301.8 2.3 multiply_convert_fusion
  304.1 0.1 reshape.49
  304.2 0.1 reshape.47
  304.3 0.1 reshape.51
  304.4 0.1 reshape.50
  304.5 0.1 reshape.48
  304.6 0.1 reshape_reshape.3
  304.7 4.7 %convolution_multiply_fusion.1 = f32[2048,1024]{1,0:T(8,128)} fusion(bf16[128,2048]{1,0:T(8,128)(2,1)S(1)} %reshape.49, bf16[128,1024]{1,0:T(8,128)(2,1)S(1)} %reshape.50), kind=kOutput, calls=%fused_computation.5 | convolution fusion | flops 538968064 | bytes 9175040 | tf_op jit(solution)/shard_map/dot_general | solution.py:144
  309.3 4.7 %convolution_multiply_fusion.2 = f32[2048,1024]{1,0:T(8,128)} fusion(bf16[128,2048]{1,0:T(8,128)(2,1)S(1)} %reshape.47, bf16[128,1024]{1,0:T(8,128)(2,1)S(1)} %reshape.48), kind=kOutput, calls=%fused_computation.6 | convolution fusion | flops 538968064 | bytes 9175040 | tf_op jit(solution)/shard_map/dot_general | solution.py:138
  314.0 4.7 %convolution_multiply_fusion = f32[1024,2048]{1,0:T(8,128)} fusion(bf16[128,1024]{1,0:T(8,128)(2,1)S(1)} %reshape_reshape.3, bf16[128,2048]{1,0:T(8,128)(2,1)S(1)} %reshape.51), kind=kOutput, calls=%fused_computation.4 | convolution fusion | flops 538968064 | bytes 9175040 | tf_op jit(solution)/shard_map/dot_general | solution.py:150
  318.7 45.0 %reduce-scatter.5.cloned.1.call-done = bf16[32,2048]{1,0:T(8,128)(2,1)} async-done(((bf16[512,2048]{1,0:T(8,128)(2,1)}), bf16[32,2048]{1,0:T(8,128)(2,1)}) %reduce-scatter.5.cloned.1.call-update) | async-done | bytes 131088 | tf_op jit(solution)/shard_map/reduce_scatter | solution.py:111
  (24 shorter events, 0.1 us)
Async XLA Ops:
  7.2 47.2 %all-gather.3.cloned.1.call-start = ((), (), s32[]{:S(2)}) async-start(), calls=%async_computation.5 | async-start | bytes 2228224 | tf_op jit(solution)/shard_map/all_gather | solution.py:69
  7.9 56.4 %copy-start.6 = (bf16[2,4,16384]{2,1,0:T(4,128)(2,1)S(1)}, bf16[2,4,16384]{2,1,0:T(4,128)(2,1)}, u32[]{:S(2)}) copy-start(bf16[2,4,16384]{2,1,0:T(4,128)(2,1)} %param.19) | copy-start | bytes 786436
  7.9 255.5 %reduce-scatter.3.cloned.1.call-start = ((), (), s32[]{:S(2)}) async-start(), calls=%async_computation.6 | async-start | bytes 3145728 | tf_op jit(solution)/shard_map/reduce_scatter | solution.py:72
  77.3 20.4 %copy-start.8 = (bf16[2,4,16384]{2,1,0:T(4,128)(2,1)S(1)}, bf16[2,4,16384]{2,1,0:T(4,128)(2,1)}, u32[]{:S(2)}) copy-start(bf16[2,4,16384]{2,1,0:T(4,128)(2,1)} %param.21) | copy-start | bytes 786436
  77.3 25.3 %copy-start.4 = (bf16[32,2048]{1,0:T(8,128)(2,1)S(1)}, bf16[32,2048]{1,0:T(8,128)(2,1)}, u32[]{:S(2)}) copy-start(bf16[32,2048]{1,0:T(8,128)(2,1)} %param.11) | copy-start | bytes 393220
  77.3 27.7 %copy-start.7 = (bf16[2,4,16384]{2,1,0:T(4,128)(2,1)S(1)}, bf16[2,4,16384]{2,1,0:T(4,128)(2,1)}, u32[]{:S(2)}) copy-start(bf16[2,4,16384]{2,1,0:T(4,128)(2,1)} %param.20) | copy-start | bytes 786436
  94.2 86.0 %all-to-all-start = ((bf16[16,2,4096]{2,1,0:T(2,128)(2,1)}), bf16[16,2,4096]{2,1,0:T(2,128)(2,1)S(1)}, u32[]{:S(2)}, u32[]{:S(2)}) async-start(bf16[16,2,4096]{2,1,0:T(2,128)(2,1)} %reshape.54), calls=%async_computation.1 | async-start | bytes 524288 | tf_op jit(solution)/shard_map/all_to_all | solution.py:65
  180.2 43.9 %all-to-all-start.1 = ((bf16[16,2,4096]{2,1,0:T(2,128)(2,1)}), bf16[16,2,4096]{2,1,0:T(2,128)(2,1)S(1)}, u32[]{:S(2)}, u32[]{:S(2)}) async-start(bf16[16,2,4096]{2,1,0:T(2,128)(2,1)} %reshape.52), calls=%async_computation.2 | async-start | bytes 524288 | tf_op jit(solution)/shard_map/all_to_all | solution.py:66
  183.7 105.0 %all-gather.5.cloned.1.call-start = ((), (), s32[]{:S(2)}) async-start(), calls=%async_computation.7 | async-start | bytes 1572864 | tf_op jit(solution)/shard_map/all_gather | solution.py:98
  262.3 0.7 copy-start.2
  270.0 20.3 %all-to-all-start.2 = ((bf16[16,2,4,1024]{3,2,1,0:T(4,128)(2,1)}), bf16[16,2,4,1024]{3,2,1,0:T(4,128)(2,1)S(1)}, u32[]{:S(2)}, u32[]{:S(2)}) async-start(bf16[16,2,4,1024]{3,2,1,0:T(4,128)(2,1)} %constant_dynamic-update-slice_fusion), calls=%async_computation.3 | async-start | bytes 524288 | tf_op jit(solution)/shard_map/all_to_all | solution.py:15
  276.0 87.7 %reduce-scatter.5.cloned.1.call-start = ((), (), s32[]{:S(2)}) async-start(), calls=%async_computation.8 | async-start | bytes 2228224 | tf_op jit(solution)/shard_map/reduce_scatter | solution.py:111
  288.7 5.7 %copy-start = (bf16[512,1024]{0,1:T(8,128)(2,1)S(1)}, bf16[512,1024]{0,1:T(8,128)(2,1)}, u32[]{:S(2)}) copy-start(bf16[512,1024]{0,1:T(8,128)(2,1)} %all-gather.5.cloned.1.call-done) | copy-start | bytes 3145732
  294.4 7.3 %copy-start.9 = (s32[32]{0:T(128)S(1)}, s32[32]{0:T(128)}, u32[]{:S(2)}) copy-start(s32[32]{0:T(128)} %param.12) | copy-start | bytes 388
  294.4 7.3 %copy-start.1 = (bf16[32,4,2048]{2,1,0:T(4,128)(2,1)S(1)}, bf16[32,4,2048]{2,1,0:T(4,128)(2,1)}, u32[]{:S(2)}) copy-start(bf16[32,4,2048]{2,1,0:T(4,128)(2,1)} %param.18) | copy-start | bytes 1572868
  294.4 7.3 %copy-start.5 = (bf16[32,4,2048]{2,1,0:T(4,128)(2,1)S(1)}, bf16[32,4,2048]{2,1,0:T(4,128)(2,1)}, u32[]{:S(2)}) copy-start(bf16[32,4,2048]{2,1,0:T(4,128)(2,1)} %param.17) | copy-start | bytes 1572868
  301.7 2.7 copy-start.3
Sparse Core Ops, SparseCore 0:
  10.1 44.1 all-gather.2
  64.5 30.6 reduce-scatter.2
  266.2 22.5 all-gather.4
  301.9 61.7 reduce-scatter.4
